TPU v7x, 128 devices: a whole 4x4x4 slice. The times are simulated.
128 devices in a mesh: ctx: 16 (over z, x), tp: 8 (over y, core).
Axes of the slice: x: 4, y: 4, z: 4, core: 2. Of those that a mesh axis runs over, the one named last changes fastest.
Arguments:
- hidden_in: bfloat16 [8192, 5376], P(('ctx', 'tp')), may hold values from -6 to 6
- stretch_start: int32 [1], replicated, may hold values from 1 to 1024
- pre_gain: float32 [5376], replicated, may hold values from 0.1 to 1.9
- q_weight: bfloat16 [5376, 4096], P('ctx', 'tp'), may hold values from -1 to 1
- k_weight: bfloat16 [5376, 2048], P('ctx', 'tp'), may hold values from -1 to 1
- v_weight: bfloat16 [5376, 2048], P('ctx', 'tp'), may hold values from -0.078125 to 0.078125
- o_weight: bfloat16 [4096, 5376], P('tp', 'ctx'), may hold values from -0.09375 to 0.09375
- q_gain: float32 [128], replicated, may hold values from 0.5 to 5
- k_gain: float32 [128], replicated, may hold values from 0.5 to 5
- prior_keys: bfloat16 [1024, 2048], P(None, 'tp'), may hold values from -6 to 6
- prior_values: bfloat16 [1024, 2048], P(None, 'tp'), may hold values from -6 to 6
- post_gain: float32 [5376], replicated, may hold values from 0.1 to 1.9
Outputs:
- result: bfloat16 [8192, 5376], P(('ctx', 'tp'))
All inputs are finite; a program needn't handle non-finite values.
Results may differ from a plain program's by a relative error of at most 0.013.
Values may be sent and summed in bfloat16 or wider, within the bound.
A program may use at most 128 MiB of HBM per device.

v0:
```python
import jax
import jax.numpy as jnp
from jax import lax
from jax.sharding import PartitionSpec as P

HD = 128
WINDOW = 1024
EPSILON = 1e-06
QUERY_FACTOR = 168.0 ** (-0.5)


def in_one_piece(arrays, axis, dim, along):
    ends, at = ([], 0)
    for a in arrays[:-1]:
        at += a.shape[along]
        ends.append(at)
    both = jnp.concatenate(arrays, axis=along)
    return tuple(jnp.split(lax.all_gather(both, axis, axis=dim, tiled=True), ends, axis=along))


def from_behind(value, axis, steps):
    count = lax.axis_size(axis)
    leading, last = (max(0, -steps), min(count, count - steps))
    return lax.ppermute(value, axis, [(source, source + steps) for source in range(leading, last)])


def rms_scale(inputs, scales):
    mean_sq = jnp.mean(inputs * inputs, axis=-1, keepdims=True)
    return inputs * lax.rsqrt(mean_sq + EPSILON) * scales


def rotate(inputs, positions):
    half_dim = inputs.shape[-1] // 2
    frequency = 10000.0 ** (-jnp.arange(half_dim, dtype=jnp.float32) / half_dim)
    angles = positions.astype(jnp.float32)[:, None] * frequency[None, :]
    cosines = jnp.cos(angles)[:, None, :]
    sines = jnp.sin(angles)[:, None, :]
    front = inputs[..., :half_dim]
    second = inputs[..., half_dim:]
    return jnp.concatenate(
        [front * cosines - second * sines, second * cosines + front * sines], axis=-1
    )


def local(
    hidden_in,
    stretch_start,
    pre_gain,
    q_weight,
    k_weight,
    v_weight,
    o_weight,
    q_gain,
    k_gain,
    prior_keys,
    prior_values,
    post_gain,
):
    residual_in = hidden_in.astype(jnp.float32)
    normed = rms_scale(residual_in, pre_gain).astype(jnp.bfloat16)
    block_rows = lax.all_gather(normed, "tp", axis=0, tiled=True)
    row_count = block_rows.shape[0]
    query_cols = q_weight.shape[1]
    kv_cols = k_weight.shape[1]

    def add_piece(segment):
        return jnp.dot(block_rows, segment, preferred_element_type=jnp.float32)

    segments = in_one_piece((q_weight, k_weight, v_weight), "ctx", 0, 1)
    query_raw, key_raw, value_raw = tuple((add_piece(segment) for segment in segments))
    local_heads = query_cols // HD
    local_kv = kv_cols // HD
    group = local_heads // local_kv
    chain_pos = lax.axis_index("ctx")
    positions = WINDOW + chain_pos * row_count + jnp.arange(row_count, dtype=jnp.int32)
    query = (
        rotate(rms_scale(query_raw.reshape(row_count, local_heads, HD), q_gain), positions)
        * QUERY_FACTOR
    ).astype(jnp.bfloat16)
    key_rows = (
        rotate(rms_scale(key_raw.reshape(row_count, local_kv, HD), k_gain), positions)
        .astype(jnp.bfloat16)
        .reshape(row_count, kv_cols)
    )
    value_rows = value_raw.astype(jnp.bfloat16)
    reach = WINDOW // row_count
    earlier = []
    current = (key_rows, value_rows)
    for hop_index in range(reach):
        current = from_behind((current[0], current[1]), "ctx", 1)
        earlier.append(current)
    key_parts = []
    value_parts = []
    for hop_index in range(reach - 1, -1, -1):
        source = chain_pos - (hop_index + 1)
        offset = jnp.maximum(WINDOW + source * row_count, 0)
        cached_keys = lax.dynamic_slice_in_dim(prior_keys, offset, row_count, 0)
        cached_values = lax.dynamic_slice_in_dim(prior_values, offset, row_count, 0)
        key_parts.append(jnp.where(source < 0, cached_keys, earlier[hop_index][0]))
        value_parts.append(jnp.where(source < 0, cached_values, earlier[hop_index][1]))
    key_parts.append(key_rows)
    value_parts.append(value_rows)
    span = (reach + 1) * row_count
    all_keys = jnp.concatenate(key_parts, axis=0).reshape(span, local_kv, HD)
    all_values = jnp.concatenate(value_parts, axis=0).reshape(span, local_kv, HD)
    key_anchor = WINDOW + (chain_pos - reach) * row_count
    query_grouped = query.reshape(row_count, local_kv, group, HD)
    scores = jnp.einsum(
        "qhgd,khd->hgqk", query_grouped, all_keys, preferred_element_type=jnp.float32
    )
    key_pos = key_anchor + jnp.arange(span, dtype=jnp.int32)
    first_valid = WINDOW - stretch_start[0]
    allowed = (
        (key_pos[None, :] <= positions[:, None])
        & (key_pos[None, :] > positions[:, None] - WINDOW)
        & (key_pos[None, :] >= first_valid)
    )
    scores = jnp.where(allowed[None, None, :, :], scores, jnp.float32(-1e30))
    largest = jnp.max(scores, axis=-1, keepdims=True)
    expon = jnp.exp(scores - largest)
    attn_probs = (expon / jnp.sum(expon, axis=-1, keepdims=True)).astype(jnp.bfloat16)
    attended = jnp.einsum(
        "hgqk,khd->qhgd", attn_probs, all_values, preferred_element_type=jnp.float32
    )
    attended = attended.astype(jnp.bfloat16).reshape(row_count, query_cols)
    partial_rows = jnp.dot(
        attended,
        lax.all_gather(o_weight, "ctx", axis=1, tiled=True),
        preferred_element_type=jnp.float32,
    )
    summed = lax.psum_scatter(
        partial_rows.astype(jnp.bfloat16), "tp", scatter_dimension=0, tiled=True
    ).astype(jnp.float32)
    return (residual_in + rms_scale(summed, post_gain)).astype(jnp.bfloat16)


def solution(mesh):
    return jax.shard_map(
        local,
        mesh=mesh,
        in_specs=(
            P(("ctx", "tp"), None),
            P(),
            P(),
            P("ctx", "tp"),
            P("ctx", "tp"),
            P("ctx", "tp"),
            P("tp", "ctx"),
            P(),
            P(),
            P(None, "tp"),
            P(None, "tp"),
            P(),
        ),
        out_specs=P(("ctx", "tp"), None),
        check_vma=False,
    )
```

profile of v0, /device:TPU:0, one launch (start us, length us, event | category | flops | bytes accessed | tf_op | source)
XLA Modules:
  0.0 256.0 jit_solution(17121036638809811373)
XLA Ops:
  6.5 0.0 all-gather.4.cloned.1.call-start
  6.5 1.3 fusion.15
  7.9 2.2 fusion.17
  10.1 0.0 all-gather.4.cloned.1.call-update
  10.1 0.0 all-gather.6.cloned.1.call-start
  10.1 2.1 pad_maximum_fusion.1
  12.3 0.0 all-gather.6.cloned.1.call-update
  12.3 0.0 all-gather.8.cloned.1.call-start
  12.3 0.7 all-gather.8.cloned.1.call-update
  13.0 0.0 reduce-scatter.2.cloned.1.call-start
  13.8 0.5 multiply_cosine_fusion
  14.3 0.1 copy.25
  14.4 0.1 copy.24
  14.6 1.9 and_and_fusion
  16.5 33.8 %all-gather.4.cloned.1.call-done = bf16[512,5376]{1,0:T(8,128)(2,1)} async-done(((bf16[64,5376]{1,0:T(8,128)(2,1)}), bf16[512,5376]{1,0:T(8,128)(2,1)}) %all-gather.4.cloned.1.call-update) | async-done | bytes 5505040 | tf_op jit(solution)/shard_map/all_gather | solution.py:61
  50.3 85.0 %all-gather.6.cloned.1.call-done = bf16[5376,1024]{1,0:T(8,128)(2,1)} async-done(((bf16[336,1024]{1,0:T(8,128)(2,1)}), bf16[5376,1024]{1,0:T(8,128)(2,1)}) %all-gather.6.cloned.1.call-update) | async-done | bytes 11010064 | tf_op jit(solution)/shard_map/all_gather | solution.py:18
  135.3 5.1 %fusion.20 = bf16[512,256]{1,0:T(8,128)(2,1)S(1)} fusion(bf16[512,5376]{1,0:T(8,128)(2,1)} %all-gather.4.cloned.1.call-done, bf16[5376,1024]{1,0:T(8,128)(2,1)} %all-gather.6.cloned.1.call-done), kind=kOutput, calls=%fused_computation.29 | convolution fusion | flops 1409417216 | bytes 8519680 | tf_op jit(solution)/shard_map/dot_general | solution.py:67
  140.4 0.0 copy-start.3
  140.4 0.0 copy-start.5
  140.4 4.2 %collective-permute-start = (bf16[512,256]{1,0:T(8,128)(2,1)S(1)}, bf16[512,256]{1,0:T(8,128)(2,1)}, u32[]{:S(2)}, u32[]{:S(2)}) collective-permute-start(bf16[512,256]{1,0:T(8,128)(2,1)S(1)} %fusion.20), channel_id=1, source_target_pairs={{0,8},{8,16},{16,24},{24,32},{32,40},{40,48},{48,56},{56,64},{64,7... | collective-permute-start | bytes 786440 | tf_op jit(solution)/shard_map/ppermute | solution.py:24
  144.6 0.0 copy-done.7
  144.6 3.5 %multiply_reduce_fusion.1 = (f32[512,2]{0,1:T(2,128)S(1)}, f32[512,256]{0,1:T(8,128)S(1)}) fusion(bf16[512,5376]{1,0:T(8,128)(2,1)S(1)} %copy-done.7, bf16[5376,1024]{1,0:T(8,128)(2,1)} %all-gather.6.cloned.1.call-done), kind=kOutput, calls=%fused_computation.43 | convolution fusion | flops 1409547264 | bytes 8785920 | tf_op jit(solution)/shard_map/dot_general | solution.py:67
  148.1 0.2 copy.23
  148.3 0.0 copy-done.3
  148.3 0.0 copy-done.5
  148.4 0.2 multiply_multiply_fusion.1
  148.6 0.2 multiply_subtract_fusion.1
  148.8 0.8 copy_bitcast_fusion
  149.7 0.0 copy-start.6
  149.7 3.5 %collective-permute-start.2 = (bf16[512,256]{1,0:T(8,128)(2,1)}, bf16[512,256]{1,0:T(8,128)(2,1)}, u32[]{:S(2)}, u32[]{:S(2)}) collective-permute-start(bf16[512,256]{1,0:T(8,128)(2,1)} %copy_bitcast_fusion), channel_id=1, source_target_pairs={{0,8},{8,16},{16,24},{24,32},{32,40},{40,48},{48,56},{56,64},{64,7... | collective-permute-start | bytes 786440 | tf_op jit(solution)/shard_map/ppermute | solution.py:24
  153.2 6.8 %multiply_reduce_fusion = (f32[512,4]{0,1:T(4,128)S(1)}, f32[512,512]{0,1:T(8,128)S(1)}) fusion(bf16[512,5376]{1,0:T(8,128)(2,1)} %all-gather.4.cloned.1.call-done, bf16[5376,1024]{1,0:T(8,128)(2,1)} %all-gather.6.cloned.1.call-done), kind=kOutput, calls=%fused_computation.33 | convolution fusion | flops 2819094528 | bytes 12066816 | tf_op jit(solution)/shard_map/dot_general | solution.py:67
  160.0 0.0 copy-done.6
  160.0 0.2 multiply_multiply_fusion
  160.2 0.0 collective-permute-done
  160.2 3.1 %collective-permute-start.1 = (bf16[512,256]{1,0:T(8,128)(2,1)}, bf16[512,256]{1,0:T(8,128)(2,1)}, u32[]{:S(2)}, u32[]{:S(2)}) collective-permute-start(bf16[512,256]{1,0:T(8,128)(2,1)} %collective-permute-done), channel_id=1, source_target_pairs={{0,8},{8,16},{16,24},{24,32},{32,40},{40,48},{48,56},{56,64},{64,7... | collective-permute-start | bytes 786440 | tf_op jit(solution)/shard_map/ppermute | solution.py:24
  163.3 0.2 multiply_subtract_fusion
  163.6 0.3 copy.30
  163.9 0.3 copy.29
  164.2 0.0 copy-start.2
  164.2 0.8 maximum_convert_fusion
  165.1 0.0 collective-permute-done.2
  165.1 3.2 %collective-permute-start.3 = (bf16[512,256]{1,0:T(8,128)(2,1)}, bf16[512,256]{1,0:T(8,128)(2,1)}, u32[]{:S(2)}, u32[]{:S(2)}) collective-permute-start(bf16[512,256]{1,0:T(8,128)(2,1)} %collective-permute-done.2), channel_id=1, source_target_pairs={{0,8},{8,16},{16,24},{24,32},{32,40},{40,48},{48,56},{56,64},{64,7... | collective-permute-start | bytes 786440 | tf_op jit(solution)/shard_map/ppermute | solution.py:24
  168.3 0.5 collective-permute-done.1
  168.7 1.2 dynamic-slice_select_fusion.1
  170.0 1.1 pad_maximum_fusion
  171.0 1.2 copy.36
  172.2 5.2 %collective-permute-done.3 = bf16[512,256]{1,0:T(8,128)(2,1)} collective-permute-done((bf16[512,256]{1,0:T(8,128)(2,1)}, bf16[512,256]{1,0:T(8,128)(2,1)}, u32[]{:S(2)}, u32[]{:S(2)}) %collective-permute-start.3) | collective-permute-done | bytes 262176 | tf_op jit(solution)/shard_map/ppermute | solution.py:24
  177.4 0.0 copy-done.2
  177.4 0.2 select_bitcast_fusion.1
  177.6 0.1 copy_bitcast_fusion.1
  177.7 0.0 copy-start.1
  177.7 10.2 %fusion.32 = (f32[2,2,512]{2,1,0:T(2,128)S(1)}, f32[2,2,512,1536]{2,3,1,0:T(8,128)}) fusion(pred[512,1536]{0,1:T(8,128)(4,1)} %and_and_fusion, bf16[512,2,128]{2,0,1:T(8,128)(2,1)} %maximum_convert_fusion, bf16[512,2,128]{2,0,1:T(8,128)(2,1)S(1)} %get-tuple-element.23, bf16[512,2,128]{2,0,1:T(8,128)(2,1)S(1)} %get-tuple-element.24, ...), kind=kOutput, calls=%fused_computation.67 | convolution fusion | flops 817890816 | bytes 15212544 | tf_op jit(solution)/shard_map/sub | solution.py:120
  187.9 0.0 copy-done.1
  187.9 5.8 %fusion.19 = bf16[2,128,2,512]{3,1,2,0:T(8,128)(2,1)S(1)} fusion(bf16[1536,2,128,1]{0,2,3,1:T(8,128)(2,1)S(1)} %bitcast.62, f32[2,2,512,1536]{2,3,1,0:T(8,128)} %get-tuple-element.20, f32[2,2,512]{2,1,0:T(2,128)S(1)} %get-tuple-element.19), kind=kOutput, calls=%fused_computation.28 | convolution fusion | flops 811859968 | bytes 13901824 | tf_op jit(solution)/shard_map/hgqk,khd->qhgd/dot_general | solution.py:122
  193.7 4.2 %all-gather.8.cloned.1.call-done = bf16[512,5376]{0,1:T(8,128)(2,1)} async-done(((bf16[512,336]{0,1:T(8,128)(2,1)}), bf16[512,5376]{0,1:T(8,128)(2,1)}) %all-gather.8.cloned.1.call-update) | async-done | bytes 5505040 | tf_op jit(solution)/shard_map/all_gather | solution.py:128
  197.9 7.5 %convolution_convert_fusion = bf16[512,5376]{1,0:T(8,128)(2,1)} fusion(bf16[512,512]{0,1:T(8,128)(2,1)S(1)} %bitcast.64, bf16[512,5376]{0,1:T(8,128)(2,1)} %all-gather.8.cloned.1.call-done), kind=kOutput, calls=%fused_computation.5 | convolution fusion | flops 2821324800 | bytes 11534336 | tf_op jit(solution)/shard_map/dot_general | solution.py:126
  205.5 0.0 copy-start
  205.5 0.0 copy-start.4
  205.5 0.0 reduce-scatter.2.cloned.1.call-update
  205.5 40.4 %reduce-scatter.2.cloned.1.call-done = bf16[64,5376]{1,0:T(8,128)(2,1)} async-done(((bf16[512,5376]{1,0:T(8,128)(2,1)}), bf16[64,5376]{1,0:T(8,128)(2,1)}) %reduce-scatter.2.cloned.1.call-update) | async-done | bytes 688144 | tf_op jit(solution)/shard_map/reduce_scatter | solution.py:131
  245.8 1.3 fusion.13
  247.2 0.0 copy-done
  247.2 0.0 copy-done.4
  247.2 2.3 fusion.18
  (10 shorter events, 0.1 us)
Async XLA Ops:
  6.5 43.8 %all-gather.4.cloned.1.call-start = ((), (), s32[]{:S(2)}) async-start(), calls=%async_computation.1 | async-start | bytes 6193152 | tf_op jit(solution)/shard_map/all_gather | solution.py:61
  10.1 125.2 %all-gather.6.cloned.1.call-start = ((), (), s32[]{:S(2)}) async-start(), calls=%async_computation.2 | async-start | bytes 11698176 | tf_op jit(solution)/shard_map/all_gather | solution.py:18
  12.3 185.7 %all-gather.8.cloned.1.call-start = ((), (), s32[]{:S(2)}) async-start(), calls=%async_computation.3 | async-start | bytes 5849088 | tf_op jit(solution)/shard_map/all_gather | solution.py:128
  13.0 232.8 %reduce-scatter.2.cloned.1.call-start = ((), (), s32[]{:S(2)}) async-start(), calls=%async_computation.4 | async-start | bytes 6193152 | tf_op jit(solution)/shard_map/reduce_scatter | solution.py:131
  135.3 9.4 %copy-start.7 = (bf16[512,5376]{1,0:T(8,128)(2,1)S(1)}, bf16[512,5376]{1,0:T(8,128)(2,1)}, u32[]{:S(2)}) copy-start(bf16[512,5376]{1,0:T(8,128)(2,1)} %all-gather.4.cloned.1.call-done) | copy-start | bytes 16515076
  140.4 7.9 %copy-start.3 = (bf16[512,256]{1,0:T(8,128)(2,1)}, bf16[512,256]{1,0:T(8,128)(2,1)S(1)}, u32[]{:S(2)}) copy-start(bf16[512,256]{1,0:T(8,128)(2,1)S(1)} %fusion.20) | copy-start | bytes 786436
  140.4 7.9 %copy-start.5 = (f32[128]{0:T(128)S(1)}, f32[128]{0:T(128)}, u32[]{:S(2)}) copy-start(f32[128]{0:T(128)} %param.20) | copy-start | bytes 1540
  140.4 19.8 %collective-permute-start = (bf16[512,256]{1,0:T(8,128)(2,1)S(1)}, bf16[512,256]{1,0:T(8,128)(2,1)}, u32[]{:S(2)}, u32[]{:S(2)}) collective-permute-start(bf16[512,256]{1,0:T(8,128)(2,1)S(1)} %fusion.20), channel_id=1, source_target_pairs={{0,8},{8,16},{16,24},{24,32},{32,40},{40,48},{48,56},{56,64},{64,7... | collective-permute-start | bytes 786440 | tf_op jit(solution)/shard_map/ppermute | solution.py:24
  149.7 10.3 %copy-start.6 = (f32[128]{0:T(128)S(1)}, f32[128]{0:T(128)}, u32[]{:S(2)}) copy-start(f32[128]{0:T(128)} %param.19) | copy-start | bytes 1540
  149.7 15.4 %collective-permute-start.2 = (bf16[512,256]{1,0:T(8,128)(2,1)}, bf16[512,256]{1,0:T(8,128)(2,1)}, u32[]{:S(2)}, u32[]{:S(2)}) collective-permute-start(bf16[512,256]{1,0:T(8,128)(2,1)} %copy_bitcast_fusion), channel_id=1, source_target_pairs={{0,8},{8,16},{16,24},{24,32},{32,40},{40,48},{48,56},{56,64},{64,7... | collective-permute-start | bytes 786440 | tf_op jit(solution)/shard_map/ppermute | solution.py:24
  160.2 8.5 %collective-permute-start.1 = (bf16[512,256]{1,0:T(8,128)(2,1)}, bf16[512,256]{1,0:T(8,128)(2,1)}, u32[]{:S(2)}, u32[]{:S(2)}) collective-permute-start(bf16[512,256]{1,0:T(8,128)(2,1)} %collective-permute-done), channel_id=1, source_target_pairs={{0,8},{8,16},{16,24},{24,32},{32,40},{40,48},{48,56},{56,64},{64,7... | collective-permute-start | bytes 786440 | tf_op jit(solution)/shard_map/ppermute | solution.py:24
  164.2 13.2 %copy-start.2 = (bf16[1024,256]{1,0:T(8,128)(2,1)S(1)}, bf16[1024,256]{1,0:T(8,128)(2,1)}, u32[]{:S(2)}) copy-start(bf16[1024,256]{1,0:T(8,128)(2,1)} %param.21) | copy-start | bytes 1572868
  165.1 12.3 %collective-permute-start.3 = (bf16[512,256]{1,0:T(8,128)(2,1)}, bf16[512,256]{1,0:T(8,128)(2,1)}, u32[]{:S(2)}, u32[]{:S(2)}) collective-permute-start(bf16[512,256]{1,0:T(8,128)(2,1)} %collective-permute-done.2), channel_id=1, source_target_pairs={{0,8},{8,16},{16,24},{24,32},{32,40},{40,48},{48,56},{56,64},{64,7... | collective-permute-start | bytes 786440 | tf_op jit(solution)/shard_map/ppermute | solution.py:24
  177.7 10.2 %copy-start.1 = (bf16[1536,256]{0,1:T(8,128)(2,1)S(1)}, bf16[1536,256]{0,1:T(8,128)(2,1)}, u32[]{:S(2)}) copy-start(bf16[1536,256]{0,1:T(8,128)(2,1)} %copy.36) | copy-start | bytes 2359300
  205.5 41.7 %copy-start = (bf16[64,5376]{1,0:T(8,128)(2,1)S(1)}, bf16[64,5376]{1,0:T(8,128)(2,1)}, u32[]{:S(2)}) copy-start(bf16[64,5376]{1,0:T(8,128)(2,1)} %param.12) | copy-start | bytes 2064388
  205.5 41.7 %copy-start.4 = (f32[5376]{0:T(1024)S(1)}, f32[5376]{0:T(1024)}, u32[]{:S(2)}) copy-start(f32[5376]{0:T(1024)} %param.23) | copy-start | bytes 64516
Sparse Core Ops, SparseCore 0:
  10.2 40.0 all-gather.3
  52.4 82.7 all-gather.5
  137.4 60.4 all-gather.7
  205.6 40.1 reduce-scatter.1
where the time goes:
time: 257 us; the launch traced here: 256 us
  waiting for transfers between devices  170 us (66%)
  matrix products  38.9 us (15%)
  other arithmetic  16.7 us (6%)
  starting transfers between devices  14.1 us (5%)
  between operations  14 us (5%)
    all_gather x1, waiting for transfers between devices, in_one_piece(): lax.all_gather(both, axis, axis=dim, tiled=True)  85 us
    reduce_scatter x1, waiting for transfers between devices, local(): lax.psum_scatter(partial_rows.astype(jnp.bfloat16), 'tp', scatter_dimensi...  40.4 us
    all_gather x1, waiting for transfers between devices, local(): block_rows = lax.all_gather(normed, 'tp', axis=0, tiled=True)  33.8 us
    dot_general x3, matrix products, add_piece(): return jnp.dot(block_rows, segment, preferred_element_type=jnp.float32)  15.4 us
    ppermute x4, starting transfers between devices, from_behind(): lax.ppermute(value, axis, [(source, source + steps) for source in range(l...  14 us
    sub x1, matrix products, local(): expon = jnp.exp(scores - largest)  10.2 us
    dot_general x1, matrix products, local(): jnp.dot(attended, lax.all_gather(o_weight, 'ctx', axis=1, tiled=True), pr...  7.51 us
    dot_general x1, matrix products, local(): jnp.einsum('hgqk,khd->qhgd', attn_probs, all_values, preferred_element_ty...  5.77 us
  transfers between devices with their start and end apart: 8, of which 6 were waited for; matrix products, arithmetic and copies ran while one was open for 17% of the time, Pallas kernels for 0%

commit v1 on v0

--- a/solution.py
+++ b/solution.py
@@ -58,7 +58,12 @@
 ):
     residual_in = hidden_in.astype(jnp.float32)
     normed = rms_scale(residual_in, pre_gain).astype(jnp.bfloat16)
-    block_rows = lax.all_gather(normed, "tp", axis=0, tiled=True)
+    ring = [normed]
+    for hop in range(7):
+        ring.append(lax.ppermute(ring[-1], "tp", [(dev, (dev + 1) % 8) for dev in range(8)]))
+    block_rows = jnp.roll(
+        jnp.concatenate(ring[::-1], axis=0), (lax.axis_index("tp") + 1) * ring[0].shape[0], axis=0
+    )
     row_count = block_rows.shape[0]
     query_cols = q_weight.shape[1]
     kv_cols = k_weight.shape[1]

time: 257 us -> 241 us (0.938)
  waiting for transfers between devices: 170 us -> 128 us
  local copies, waits for them, and re-layouts: 2.41 us -> 22.9 us
  other arithmetic: 16.7 us -> 19.7 us
    all_gather x1, waiting for transfers between devices: 85 us -> 0.01 us  [in_one_piece(): lax.all_gather(both, axis, axis=dim, tiled=True)]
    ppermute x0 -> x7, waiting for transfers between devices: none -> 74.2 us  [local(): lax.ppermute(ring[-1], 'tp', [(dev, (dev + 1) % 8) for dev in range(8)])]
    all_gather x1 -> x0, waiting for transfers between devices: 33.8 us -> none  [local(): block_rows = lax.all_gather(normed, 'tp', axis=0, tiled=True)]
    unnamed x16 -> x34, local copies, waits for them, and re-layouts: 0.04 us -> 17.2 us
    ppermute x4, waiting for transfers between devices: 5.67 us -> 12 us  [from_behind(): lax.ppermute(value, axis, [(source, source + steps) for source in range(l...]
    all_gather x1, waiting for transfers between devices: 4.23 us -> 0.02 us  [local(): lax.all_gather(o_weight, 'ctx', axis=1, tiled=True)]
  transfers between devices with their start and end apart: 8 -> 14, of which waited for: 6 -> 10; matrix products, arithmetic and copies ran while one was open for 17% -> 29% of each run, Pallas kernels for 0% -> 0%
where the time goes in v1:
time: 241 us; the launch traced here: 240 us
  waiting for transfers between devices  128 us (53%)
  matrix products  40.4 us (17%)
  local copies, waits for them, and re-layouts  22.9 us (10%)
  other arithmetic  19.7 us (8%)
  starting transfers between devices  15.1 us (6%)
  between operations  14.1 us (6%)
    ppermute x7, waiting for transfers between devices, local(): lax.ppermute(ring[-1], 'tp', [(dev, (dev + 1) % 8) for dev in range(8)])  74.2 us
    reduce_scatter x1, waiting for transfers between devices, local(): lax.psum_scatter(partial_rows.astype(jnp.bfloat16), 'tp', scatter_dimensi...  41.5 us
    unnamed x34, local copies, waits for them, and re-layouts  17.2 us
    dot_general x3, matrix products, add_piece(): return jnp.dot(block_rows, segment, preferred_element_type=jnp.float32)  16.9 us
    ppermute x4, starting transfers between devices, from_behind(): lax.ppermute(value, axis, [(source, source + steps) for source in range(l...  15 us
    ppermute x4, waiting for transfers between devices, from_behind(): lax.ppermute(value, axis, [(source, source + steps) for source in range(l...  12 us
    sub x1, matrix products, local(): expon = jnp.exp(scores - largest)  10.4 us
    dot_general x1, matrix products, local(): jnp.dot(attended, lax.all_gather(o_weight, 'ctx', axis=1, tiled=True), pr...  7.51 us
  transfers between devices with their start and end apart: 14, of which 10 were waited for; matrix products, arithmetic and copies ran while one was open for 29% of the time, Pallas kernels for 0%

profile of v1, /device:TPU:0, one launch (start us, length us, event | category | flops | bytes accessed | tf_op | source)
XLA Modules:
  0.0 240.0 jit_solution(1282670732980351935)
XLA Ops:
  6.5 2.1 pad_maximum_fusion.1
  8.7 0.0 all-gather.5.cloned.1.call-start
  8.8 1.3 fusion.18
  10.1 1.3 fusion.20
  11.5 0.0 collective-permute-start
  11.5 11.6 %collective-permute-done = bf16[64,5376]{1,0:T(8,128)(2,1)S(1)} collective-permute-done((bf16[64,5376]{1,0:T(8,128)(2,1)S(1)}, bf16[64,5376]{1,0:T(8,128)(2,1)S(1)}, u32[]{:S(2)}, u32[]{:S(2)}) %collective-permute-start) | collective-permute-done | bytes 688160 | tf_op jit(solution)/shard_map/ppermute | solution.py:63
  23.0 11.6 %collective-permute-done.1 = bf16[64,5376]{1,0:T(8,128)(2,1)S(1)} collective-permute-done((bf16[64,5376]{1,0:T(8,128)(2,1)S(1)}, bf16[64,5376]{1,0:T(8,128)(2,1)S(1)}, u32[]{:S(2)}, u32[]{:S(2)}) %collective-permute-start.1) | collective-permute-done | bytes 688160 | tf_op jit(solution)/shard_map/ppermute | solution.py:63
  34.6 11.6 %collective-permute-done.2 = bf16[64,5376]{1,0:T(8,128)(2,1)S(1)} collective-permute-done((bf16[64,5376]{1,0:T(8,128)(2,1)S(1)}, bf16[64,5376]{1,0:T(8,128)(2,1)S(1)}, u32[]{:S(2)}, u32[]{:S(2)}) %collective-permute-start.2) | collective-permute-done | bytes 688160 | tf_op jit(solution)/shard_map/ppermute | solution.py:63
  46.2 11.6 %collective-permute-done.3 = bf16[64,5376]{1,0:T(8,128)(2,1)S(1)} collective-permute-done((bf16[64,5376]{1,0:T(8,128)(2,1)S(1)}, bf16[64,5376]{1,0:T(8,128)(2,1)S(1)}, u32[]{:S(2)}, u32[]{:S(2)}) %collective-permute-start.3) | collective-permute-done | bytes 688160 | tf_op jit(solution)/shard_map/ppermute | solution.py:63
  57.8 11.7 %collective-permute-done.4 = bf16[64,5376]{1,0:T(8,128)(2,1)} collective-permute-done((bf16[64,5376]{1,0:T(8,128)(2,1)S(1)}, bf16[64,5376]{1,0:T(8,128)(2,1)}, u32[]{:S(2)}, u32[]{:S(2)}) %collective-permute-start.4) | collective-permute-done | bytes 688160 | tf_op jit(solution)/shard_map/ppermute | solution.py:63
  69.4 0.0 all-gather.5.cloned.1.call-update
  69.5 0.0 reduce-scatter.2.cloned.1.call-start
  70.2 1.2 multiply_cosine_fusion
  71.5 1.8 copy.25
  73.2 1.8 copy.24
  75.0 6.3 %collective-permute-done.5 = bf16[64,5376]{1,0:T(8,128)(2,1)} collective-permute-done((bf16[64,5376]{1,0:T(8,128)(2,1)}, bf16[64,5376]{1,0:T(8,128)(2,1)}, u32[]{:S(2)}, u32[]{:S(2)}) %collective-permute-start.5) | collective-permute-done | bytes 688160 | tf_op jit(solution)/shard_map/ppermute | solution.py:63
  81.4 1.9 and_and_fusion
  83.2 9.9 %collective-permute-done.6 = bf16[64,5376]{1,0:T(8,128)(2,1)S(1)} collective-permute-done((bf16[64,5376]{1,0:T(8,128)(2,1)}, bf16[64,5376]{1,0:T(8,128)(2,1)S(1)}, u32[]{:S(2)}, u32[]{:S(2)}) %collective-permute-start.6) | collective-permute-done | bytes 688160 | tf_op jit(solution)/shard_map/ppermute | solution.py:63
  93.1 0.9 constant_dynamic-update-slice_fusion.15
  94.0 2.0 constant_dynamic-update-slice_fusion.14
  96.0 2.0 constant_dynamic-update-slice_fusion.13
  98.0 0.9 constant_dynamic-update-slice_fusion.12
  99.0 0.9 constant_dynamic-update-slice_fusion.11
  99.9 0.9 constant_dynamic-update-slice_fusion.10
  100.7 0.9 constant_dynamic-update-slice_fusion.9
  101.7 1.1 constant_dynamic-update-slice_fusion.8
  102.7 0.9 constant_dynamic-update-slice_fusion.7
  103.7 2.0 constant_dynamic-update-slice_fusion.6
  105.6 2.1 constant_dynamic-update-slice_fusion.5
  107.7 0.9 constant_dynamic-update-slice_fusion.4
  108.6 0.9 constant_dynamic-update-slice_fusion.3
  109.5 0.9 constant_dynamic-update-slice_fusion.2
  110.4 0.9 constant_dynamic-update-slice_fusion.1
  111.3 1.1 constant_dynamic-update-slice_fusion
  112.4 5.1 %fusion.23 = bf16[512,256]{1,0:T(8,128)(2,1)S(1)} fusion(bf16[5376,1024]{1,0:T(8,128)(2,1)} %all-gather.3.cloned.1.call-done, bf16[1024,5376]{1,0:T(8,128)(2,1)} %constant_dynamic-update-slice_fusion, s32[]{:T(128)S(6)} %select_n.45), kind=kOutput, calls=%fused_computation.32 | convolution fusion | flops 1409417216 | bytes 8519684 | tf_op jit(solution)/shard_map/dot_general | solution.py:72
  117.6 4.2 %collective-permute-start.7 = (bf16[512,256]{1,0:T(8,128)(2,1)S(1)}, bf16[512,256]{1,0:T(8,128)(2,1)}, u32[]{:S(2)}, u32[]{:S(2)}) collective-permute-start(bf16[512,256]{1,0:T(8,128)(2,1)S(1)} %fusion.23), channel_id=1, source_target_pairs={{0,8},{8,16},{16,24},{24,32},{32,40},{40,48},{48,56},{56,64},{64,7... | collective-permute-start | bytes 786440 | tf_op jit(solution)/shard_map/ppermute | solution.py:24
  121.8 5.1 %multiply_reduce_fusion.1 = (f32[512,2]{0,1:T(2,128)S(1)}, f32[512,256]{0,1:T(8,128)S(1)}) fusion(bf16[5376,1024]{1,0:T(8,128)(2,1)} %all-gather.3.cloned.1.call-done, bf16[1024,5376]{1,0:T(8,128)(2,1)} %constant_dynamic-update-slice_fusion, s32[]{:T(128)S(6)} %select_n.45), kind=kOutput, calls=%fused_computation.46 | convolution fusion | flops 1409547264 | bytes 8785924 | tf_op jit(solution)/shard_map/dot_general | solution.py:72
  126.8 0.2 copy.23
  127.0 0.2 multiply_multiply_fusion.1
  127.3 0.2 multiply_subtract_fusion.1
  127.5 0.8 copy_bitcast_fusion
  128.4 3.5 %collective-permute-start.9 = (bf16[512,256]{1,0:T(8,128)(2,1)}, bf16[512,256]{1,0:T(8,128)(2,1)}, u32[]{:S(2)}, u32[]{:S(2)}) collective-permute-start(bf16[512,256]{1,0:T(8,128)(2,1)} %copy_bitcast_fusion), channel_id=1, source_target_pairs={{0,8},{8,16},{16,24},{24,32},{32,40},{40,48},{48,56},{56,64},{64,7... | collective-permute-start | bytes 786440 | tf_op jit(solution)/shard_map/ppermute | solution.py:24
  131.9 6.7 %multiply_reduce_fusion = (f32[512,4]{0,1:T(4,128)S(1)}, f32[512,512]{0,1:T(8,128)S(1)}) fusion(bf16[5376,1024]{1,0:T(8,128)(2,1)} %all-gather.3.cloned.1.call-done, bf16[1024,5376]{1,0:T(8,128)(2,1)} %constant_dynamic-update-slice_fusion, s32[]{:T(128)S(6)} %select_n.45), kind=kOutput, calls=%fused_computation.36 | convolution fusion | flops 2819094528 | bytes 12066820 | tf_op jit(solution)/shard_map/dot_general | solution.py:72
  138.7 0.2 multiply_multiply_fusion
  138.9 3.1 %collective-permute-start.8 = (bf16[512,256]{1,0:T(8,128)(2,1)}, bf16[512,256]{1,0:T(8,128)(2,1)}, u32[]{:S(2)}, u32[]{:S(2)}) collective-permute-start(bf16[512,256]{1,0:T(8,128)(2,1)} %collective-permute-done.7), channel_id=1, source_target_pairs={{0,8},{8,16},{16,24},{24,32},{32,40},{40,48},{48,56},{56,64},{64,7... | collective-permute-start | bytes 786440 | tf_op jit(solution)/shard_map/ppermute | solution.py:24
  142.1 0.2 multiply_subtract_fusion
  142.2 0.3 copy.30
  142.6 1.4 copy.29
  143.9 0.8 maximum_convert_fusion
  144.8 4.1 %collective-permute-start.10 = (bf16[512,256]{1,0:T(8,128)(2,1)}, bf16[512,256]{1,0:T(8,128)(2,1)}, u32[]{:S(2)}, u32[]{:S(2)}) collective-permute-start(bf16[512,256]{1,0:T(8,128)(2,1)} %collective-permute-done.9), channel_id=1, source_target_pairs={{0,8},{8,16},{16,24},{24,32},{32,40},{40,48},{48,56},{56,64},{64,7... | collective-permute-start | bytes 786440 | tf_op jit(solution)/shard_map/ppermute | solution.py:24
  148.9 6.1 %collective-permute-done.8 = bf16[512,256]{1,0:T(8,128)(2,1)} collective-permute-done((bf16[512,256]{1,0:T(8,128)(2,1)}, bf16[512,256]{1,0:T(8,128)(2,1)}, u32[]{:S(2)}, u32[]{:S(2)}) %collective-permute-start.8) | collective-permute-done | bytes 262176 | tf_op jit(solution)/shard_map/ppermute | solution.py:24
  155.0 1.2 dynamic-slice_select_fusion.1
  156.2 1.0 pad_maximum_fusion
  157.2 0.3 copy.36
  157.5 5.9 %collective-permute-done.10 = bf16[512,256]{1,0:T(8,128)(2,1)} collective-permute-done((bf16[512,256]{1,0:T(8,128)(2,1)}, bf16[512,256]{1,0:T(8,128)(2,1)}, u32[]{:S(2)}, u32[]{:S(2)}) %collective-permute-start.10) | collective-permute-done | bytes 262176 | tf_op jit(solution)/shard_map/ppermute | solution.py:24
  163.4 1.2 select_bitcast_fusion.1
  164.6 0.1 copy_bitcast_fusion.1
  164.7 10.4 %fusion.40 = (f32[2,2,512]{2,1,0:T(2,128)S(1)}, f32[2,2,512,1536]{2,3,1,0:T(8,128)}) fusion(pred[512,1536]{0,1:T(8,128)(4,1)} %and_and_fusion, bf16[512,2,128]{2,0,1:T(8,128)(2,1)} %maximum_convert_fusion, bf16[512,2,128]{2,0,1:T(8,128)(2,1)S(1)} %get-tuple-element.23, bf16[512,2,128]{2,0,1:T(8,128)(2,1)S(1)} %get-tuple-element.24, ...), kind=kOutput, calls=%fused_computation.89 | convolution fusion | flops 817890816 | bytes 15212544 | tf_op jit(solution)/shard_map/sub | solution.py:125
  175.2 5.6 %fusion.22 = bf16[2,128,2,512]{3,1,2,0:T(8,128)(2,1)S(1)} fusion(bf16[1536,2,128,1]{0,2,3,1:T(8,128)(2,1)S(1)} %bitcast.59, f32[2,2,512,1536]{2,3,1,0:T(8,128)} %get-tuple-element.20, f32[2,2,512]{2,1,0:T(2,128)S(1)} %get-tuple-element.19), kind=kOutput, calls=%fused_computation.31 | convolution fusion | flops 811859968 | bytes 13901824 | tf_op jit(solution)/shard_map/hgqk,khd->qhgd/dot_general | solution.py:127
  180.8 0.0 all-gather.5.cloned.1.call-done
  180.8 7.5 %convolution_convert_fusion = bf16[512,5376]{1,0:T(8,128)(2,1)} fusion(bf16[512,512]{0,1:T(8,128)(2,1)S(1)} %bitcast.61, bf16[512,5376]{0,1:T(8,128)(2,1)} %all-gather.5.cloned.1.call-done), kind=kOutput, calls=%fused_computation.5 | convolution fusion | flops 2821324800 | bytes 11534336 | tf_op jit(solution)/shard_map/dot_general | solution.py:131
  188.3 41.5 %reduce-scatter.2.cloned.1.call-done = bf16[64,5376]{1,0:T(8,128)(2,1)} async-done(((bf16[512,5376]{1,0:T(8,128)(2,1)}), bf16[64,5376]{1,0:T(8,128)(2,1)}) %reduce-scatter.2.cloned.1.call-update) | async-done | bytes 688144 | tf_op jit(solution)/shard_map/reduce_scatter | solution.py:136
  229.8 1.3 fusion.16
  231.2 2.3 fusion.21
  (41 shorter events, 0.2 us)
Async XLA Ops:
  6.5 95.1 %copy-start = (bf16[64,5376]{1,0:T(8,128)(2,1)S(1)}, bf16[64,5376]{1,0:T(8,128)(2,1)}, u32[]{:S(2)}) copy-start(bf16[64,5376]{1,0:T(8,128)(2,1)} %param.12) | copy-start | bytes 2064388
  6.5 95.1 %copy-start.6 = (f32[5376]{0:T(1024)S(1)}, f32[5376]{0:T(1024)}, u32[]{:S(2)}) copy-start(f32[5376]{0:T(1024)} %param.14) | copy-start | bytes 64516
  6.5 105.9 %all-gather.3.cloned.1.call-start = ((), (), s32[]{:S(2)}) async-start(), calls=%async_computation.1 | async-start | bytes 11698176 | tf_op jit(solution)/shard_map/all_gather | solution.py:18
  8.7 172.1 %all-gather.5.cloned.1.call-start = ((), (), s32[]{:S(2)}) async-start(), calls=%async_computation.2 | async-start | bytes 5849088 | tf_op jit(solution)/shard_map/all_gather | solution.py:133
  11.5 11.6 %collective-permute-start = (bf16[64,5376]{1,0:T(8,128)(2,1)S(1)}, bf16[64,5376]{1,0:T(8,128)(2,1)S(1)}, u32[]{:S(2)}, u32[]{:S(2)}) collective-permute-start(bf16[64,5376]{1,0:T(8,128)(2,1)S(1)} %fusion.20), channel_id=1, source_target_pairs={{0,1},{1,2},{2,3},{3,4},{4,5},{5,6},{6,7},{7,0},{8,9},{9,10},{10,1... | collective-permute-start | bytes 2064392 | tf_op jit(solution)/shard_map/ppermute | solution.py:63
  23.0 11.6 %collective-permute-start.1 = (bf16[64,5376]{1,0:T(8,128)(2,1)S(1)}, bf16[64,5376]{1,0:T(8,128)(2,1)S(1)}, u32[]{:S(2)}, u32[]{:S(2)}) collective-permute-start(bf16[64,5376]{1,0:T(8,128)(2,1)S(1)} %collective-permute-done), channel_id=1, source_target_pairs={{0,1},{1,2},{2,3},{3,4},{4,5},{5,6},{6,7},{7,0},{8,9},{9,10},{10,1... | collective-permute-start | bytes 2064392 | tf_op jit(solution)/shard_map/ppermute | solution.py:63
  34.6 11.6 %collective-permute-start.2 = (bf16[64,5376]{1,0:T(8,128)(2,1)S(1)}, bf16[64,5376]{1,0:T(8,128)(2,1)S(1)}, u32[]{:S(2)}, u32[]{:S(2)}) collective-permute-start(bf16[64,5376]{1,0:T(8,128)(2,1)S(1)} %collective-permute-done.1), channel_id=1, source_target_pairs={{0,1},{1,2},{2,3},{3,4},{4,5},{5,6},{6,7},{7,0},{8,9},{9,10},{10,1... | collective-permute-start | bytes 2064392 | tf_op jit(solution)/shard_map/ppermute | solution.py:63
  46.2 11.6 %collective-permute-start.3 = (bf16[64,5376]{1,0:T(8,128)(2,1)S(1)}, bf16[64,5376]{1,0:T(8,128)(2,1)S(1)}, u32[]{:S(2)}, u32[]{:S(2)}) collective-permute-start(bf16[64,5376]{1,0:T(8,128)(2,1)S(1)} %collective-permute-done.2), channel_id=1, source_target_pairs={{0,1},{1,2},{2,3},{3,4},{4,5},{5,6},{6,7},{7,0},{8,9},{9,10},{10,1... | collective-permute-start | bytes 2064392 | tf_op jit(solution)/shard_map/ppermute | solution.py:63
  57.8 11.7 %collective-permute-start.4 = (bf16[64,5376]{1,0:T(8,128)(2,1)S(1)}, bf16[64,5376]{1,0:T(8,128)(2,1)}, u32[]{:S(2)}, u32[]{:S(2)}) collective-permute-start(bf16[64,5376]{1,0:T(8,128)(2,1)S(1)} %collective-permute-done.3), channel_id=1, source_target_pairs={{0,1},{1,2},{2,3},{3,4},{4,5},{5,6},{6,7},{7,0},{8,9},{9,10},{10,1... | collective-permute-start | bytes 2064392 | tf_op jit(solution)/shard_map/ppermute | solution.py:63
  69.4 11.9 %collective-permute-start.5 = (bf16[64,5376]{1,0:T(8,128)(2,1)}, bf16[64,5376]{1,0:T(8,128)(2,1)}, u32[]{:S(2)}, u32[]{:S(2)}) collective-permute-start(bf16[64,5376]{1,0:T(8,128)(2,1)} %collective-permute-done.4), channel_id=1, source_target_pairs={{0,1},{1,2},{2,3},{3,4},{4,5},{5,6},{6,7},{7,0},{8,9},{9,10},{10,1... | collective-permute-start | bytes 2064392 | tf_op jit(solution)/shard_map/ppermute | solution.py:63
  69.5 160.4 %reduce-scatter.2.cloned.1.call-start = ((), (), s32[]{:S(2)}) async-start(), calls=%async_computation.3 | async-start | bytes 6193152 | tf_op jit(solution)/shard_map/reduce_scatter | solution.py:136
  81.3 11.8 %collective-permute-start.6 = (bf16[64,5376]{1,0:T(8,128)(2,1)}, bf16[64,5376]{1,0:T(8,128)(2,1)S(1)}, u32[]{:S(2)}, u32[]{:S(2)}) collective-permute-start(bf16[64,5376]{1,0:T(8,128)(2,1)} %collective-permute-done.5), channel_id=1, source_target_pairs={{0,1},{1,2},{2,3},{3,4},{4,5},{5,6},{6,7},{7,0},{8,9},{9,10},{10,1... | collective-permute-start | bytes 2064392 | tf_op jit(solution)/shard_map/ppermute | solution.py:63
  112.4 14.6 %copy-start.8 = (f32[128]{0:T(128)S(1)}, f32[128]{0:T(128)}, u32[]{:S(2)}) copy-start(f32[128]{0:T(128)} %param.20) | copy-start | bytes 1540
  112.4 14.8 %copy-start.3 = (f32[512,64]{1,0:T(8,128)S(1)}, f32[512,64]{1,0:T(8,128)}, u32[]{:S(2)}) copy-start(f32[512,64]{1,0:T(8,128)} %copy.25) | copy-start | bytes 393220
  112.4 14.9 %copy-start.4 = (f32[512,64]{1,0:T(8,128)S(1)}, f32[512,64]{1,0:T(8,128)}, u32[]{:S(2)}) copy-start(f32[512,64]{1,0:T(8,128)} %copy.24) | copy-start | bytes 393220
  117.6 21.1 %copy-start.5 = (bf16[512,256]{1,0:T(8,128)(2,1)}, bf16[512,256]{1,0:T(8,128)(2,1)S(1)}, u32[]{:S(2)}) copy-start(bf16[512,256]{1,0:T(8,128)(2,1)S(1)} %fusion.23) | copy-start | bytes 786436
  117.6 21.3 %collective-permute-start.7 = (bf16[512,256]{1,0:T(8,128)(2,1)S(1)}, bf16[512,256]{1,0:T(8,128)(2,1)}, u32[]{:S(2)}, u32[]{:S(2)}) collective-permute-start(bf16[512,256]{1,0:T(8,128)(2,1)S(1)} %fusion.23), channel_id=1, source_target_pairs={{0,8},{8,16},{16,24},{24,32},{32,40},{40,48},{48,56},{56,64},{64,7... | collective-permute-start | bytes 786440 | tf_op jit(solution)/shard_map/ppermute | solution.py:24
  127.5 11.2 %copy-start.9 = (f32[128]{0:T(128)S(1)}, f32[128]{0:T(128)}, u32[]{:S(2)}) copy-start(f32[128]{0:T(128)} %param.19) | copy-start | bytes 1540
  128.4 13.7 %copy-start.1 = (f32[512,64]{0,1:T(8,128)S(1)}, f32[512,64]{0,1:T(8,128)}, u32[]{:S(2)}) copy-start(f32[512,64]{0,1:T(8,128)} %get-tuple-element.13) | copy-start | bytes 393220
  128.4 13.7 %copy-start.2 = (f32[512,64]{0,1:T(8,128)S(1)}, f32[512,64]{0,1:T(8,128)}, u32[]{:S(2)}) copy-start(f32[512,64]{0,1:T(8,128)} %get-tuple-element.14) | copy-start | bytes 393220
  128.4 16.4 %collective-permute-start.9 = (bf16[512,256]{1,0:T(8,128)(2,1)}, bf16[512,256]{1,0:T(8,128)(2,1)}, u32[]{:S(2)}, u32[]{:S(2)}) collective-permute-start(bf16[512,256]{1,0:T(8,128)(2,1)} %copy_bitcast_fusion), channel_id=1, source_target_pairs={{0,8},{8,16},{16,24},{24,32},{32,40},{40,48},{48,56},{56,64},{64,7... | collective-permute-start | bytes 786440 | tf_op jit(solution)/shard_map/ppermute | solution.py:24
  138.9 16.1 %collective-permute-start.8 = (bf16[512,256]{1,0:T(8,128)(2,1)}, bf16[512,256]{1,0:T(8,128)(2,1)}, u32[]{:S(2)}, u32[]{:S(2)}) collective-permute-start(bf16[512,256]{1,0:T(8,128)(2,1)} %collective-permute-done.7), channel_id=1, source_target_pairs={{0,8},{8,16},{16,24},{24,32},{32,40},{40,48},{48,56},{56,64},{64,7... | collective-permute-start | bytes 786440 | tf_op jit(solution)/shard_map/ppermute | solution.py:24
  144.8 18.6 %collective-permute-start.10 = (bf16[512,256]{1,0:T(8,128)(2,1)}, bf16[512,256]{1,0:T(8,128)(2,1)}, u32[]{:S(2)}, u32[]{:S(2)}) collective-permute-start(bf16[512,256]{1,0:T(8,128)(2,1)} %collective-permute-done.9), channel_id=1, source_target_pairs={{0,8},{8,16},{16,24},{24,32},{32,40},{40,48},{48,56},{56,64},{64,7... | collective-permute-start | bytes 786440 | tf_op jit(solution)/shard_map/ppermute | solution.py:24
  180.8 50.4 %copy-start.7 = (f32[5376]{0:T(1024)S(1)}, f32[5376]{0:T(1024)}, u32[]{:S(2)}) copy-start(f32[5376]{0:T(1024)} %param.23) | copy-start | bytes 64516
Sparse Core Ops, SparseCore 0:
  9.5 85.2 all-gather.2
  96.9 72.9 all-gather.4
  188.5 41.3 reduce-scatter.1
